TPU v7x, 32 devices: a whole 2x2x4 slice. The times are simulated.
32 devices in a mesh: dp: 2 (over core), mp: 16 (over z, y, x).
Axes of the slice: x: 2, y: 2, z: 4, core: 2. Of those that a mesh axis runs over, the one named last changes fastest.
Arguments:
- tokens: bfloat16 [512, 2048], P('dp', 'mp'), may hold values from -6 to 6
- gate_weights: bfloat16 [2, 2048, 7168], P(None, None, 'mp'), may hold values from -0.125 to 0.125
- up_weights: bfloat16 [2, 2048, 7168], P(None, None, 'mp'), may hold values from -0.125 to 0.125
- down_weights: bfloat16 [2, 7168, 2048], P(None, 'mp'), may hold values from -0.0625 to 0.0625
- rhs_gate: float32 [2, 2048, 7168], P(None, 'dp', 'mp'), may hold values from -6 to 6
- rhs_up: float32 [2, 2048, 7168], P(None, 'dp', 'mp'), may hold values from -6 to 6
- rhs_down: float32 [2, 7168, 2048], P(None, 'mp', 'dp'), may hold values from -6 to 6
- damping: float32 [1], replicated, may hold values from 0.5 to 2
Outputs:
- step_gate: float32 [2, 2048, 7168], P(None, 'dp', 'mp')
- step_up: float32 [2, 2048, 7168], P(None, 'dp', 'mp')
- step_down: float32 [2, 7168, 2048], P(None, 'mp', 'dp')
- next_gate: float32 [2, 2048, 7168], P(None, 'dp', 'mp')
- next_up: float32 [2, 2048, 7168], P(None, 'dp', 'mp')
- next_down: float32 [2, 7168, 2048], P(None, 'mp', 'dp')
All inputs are finite; a program needn't handle non-finite values.
Results may differ from a plain program's by a relative error of at most 0.007.
Values may be sent and summed in bfloat16 or wider, within the bound.
A program may use at most 128 MiB of HBM per device.

v0:
```python
import jax
import jax.numpy as jnp
from jax import lax
from jax.sharding import PartitionSpec as P

ITERS = 1


def silu_terms(value):
    sigmoid_value = jax.nn.sigmoid(value)
    return (value * sigmoid_value, sigmoid_value * (1.0 + value * (1.0 - sigmoid_value)))


def matmul(left, right):
    return jnp.dot(left, right, preferred_element_type=jnp.float32)


def rows_product(left, right):
    return lax.dot_general(
        left, right, (((0,), (0,)), ((), ())), preferred_element_type=jnp.float32
    )


def against(left, right):
    return lax.dot_general(
        left, right, (((1,), (1,)), ((), ())), preferred_element_type=jnp.float32
    )


def local_inner(first, second):
    return (
        jnp.sum(first[0] * second[0])
        + jnp.sum(first[1] * second[1])
        + jnp.sum(first[2] * second[2])
    )


def finish_first(partial_value, whole_add):
    summed = lax.psum(partial_value, "mp")
    if whole_add is not None:
        summed = summed + whole_add.astype(jnp.float32)
    return summed.astype(jnp.bfloat16)


def body(tokens, gate_weights, up_weights, down_weights, rhs_gate, rhs_up, rhs_down, damping):
    share = tokens.shape[1]
    offset = lax.axis_index("mp") * share
    total_tokens = tokens.shape[0] * lax.axis_size("dp")
    tokens_whole = lax.all_gather(tokens, "mp", axis=1, tiled=True)
    gate_one = matmul(tokens_whole, gate_weights[0])
    up_one = matmul(tokens_whole, up_weights[0])
    active_one, slope_one = silu_terms(gate_one)
    hidden_one = (active_one * up_one).astype(jnp.bfloat16)
    layer_one = finish_first(matmul(hidden_one, down_weights[0]), tokens_whole)
    gate_two = matmul(layer_one, gate_weights[1])
    up_two = matmul(layer_one, up_weights[1])
    active_two, slope_two = silu_terms(gate_two)
    hidden_two = (active_two * up_two).astype(jnp.bfloat16)

    def curvature(vectors):
        tangent_gate, tangent_up, tangent_down = (
            lax.all_gather(vectors[0].astype(jnp.bfloat16), "dp", axis=1, tiled=True),
            lax.all_gather(vectors[1].astype(jnp.bfloat16), "dp", axis=1, tiled=True),
            lax.all_gather(vectors[2].astype(jnp.bfloat16), "dp", axis=2, tiled=True),
        )
        tan_gate = matmul(tokens_whole, tangent_gate[0])
        tan_up = matmul(tokens_whole, tangent_up[0])
        tan_hidden = (slope_one * up_one * tan_gate + active_one * tan_up).astype(jnp.bfloat16)
        tan_layer = finish_first(
            matmul(tan_hidden, down_weights[0]) + matmul(hidden_one, tangent_down[0]), None
        )
        tan_gate = matmul(tan_layer, gate_weights[1]) + matmul(layer_one, tangent_gate[1])
        tan_up = matmul(tan_layer, up_weights[1]) + matmul(layer_one, tangent_up[1])
        tan_hidden = (slope_two * up_two * tan_gate + active_two * tan_up).astype(jnp.bfloat16)
        second_partial = matmul(tan_hidden, down_weights[1]) + matmul(hidden_two, tangent_down[1])
        second_summed = lax.psum_scatter(second_partial, "mp", scatter_dimension=1, tiled=True)
        layer_slice = lax.dynamic_slice_in_dim(tan_layer, offset, share, 1)
        cotan_share = (layer_slice.astype(jnp.float32) + second_summed).astype(jnp.bfloat16)
        cotan = lax.all_gather(cotan_share, "mp", axis=1, tiled=True)
        grad_down_two = rows_product(hidden_two, cotan)
        back_hidden = against(cotan, down_weights[1])
        back_gate = (back_hidden * up_two * slope_two).astype(jnp.bfloat16)
        back_up = (back_hidden * active_two).astype(jnp.bfloat16)
        grad_gate_two = rows_product(layer_one, back_gate)
        grad_up_two = rows_product(layer_one, back_up)
        back_partial = against(back_gate, gate_weights[1]) + against(back_up, up_weights[1])
        back_layer = finish_first(back_partial, cotan)
        grad_down_one = rows_product(hidden_one, back_layer)
        back_hidden = against(back_layer, down_weights[0])
        back_gate = (back_hidden * up_one * slope_one).astype(jnp.bfloat16)
        back_up = (back_hidden * active_one).astype(jnp.bfloat16)
        grad_gate_one = rows_product(tokens_whole, back_gate)
        grad_up_one = rows_product(tokens_whole, back_up)
        summed_gate, summed_up, summed_down = (
            lax.psum_scatter(
                jnp.stack([grad_gate_one, grad_gate_two]).astype(jnp.bfloat16),
                "dp",
                scatter_dimension=1,
                tiled=True,
            ).astype(jnp.float32),
            lax.psum_scatter(
                jnp.stack([grad_up_one, grad_up_two]).astype(jnp.bfloat16),
                "dp",
                scatter_dimension=1,
                tiled=True,
            ).astype(jnp.float32),
            lax.psum_scatter(
                jnp.stack([grad_down_one, grad_down_two]).astype(jnp.bfloat16),
                "dp",
                scatter_dimension=2,
                tiled=True,
            ).astype(jnp.float32),
        )
        scale = 1.0 / total_tokens
        return (
            summed_gate * scale + damping[0] * vectors[0],
            summed_up * scale + damping[0] * vectors[1],
            summed_down * scale + damping[0] * vectors[2],
        )

    residual = (rhs_gate, rhs_up, rhs_down)
    direction = residual
    solution = (jnp.zeros_like(rhs_gate), jnp.zeros_like(rhs_up), jnp.zeros_like(rhs_down))
    norm_now = lax.psum(local_inner(residual, residual), ("dp", "mp"))
    for rounds in range(ITERS):
        image = curvature(direction)
        along, crossed, squared = lax.psum(
            (
                local_inner(direction, image),
                local_inner(residual, image),
                local_inner(image, image),
            ),
            ("dp", "mp"),
        )
        alpha = norm_now / along
        solution = tuple((solution[k] + alpha * direction[k] for k in range(3)))
        residual = tuple((residual[k] - alpha * image[k] for k in range(3)))
        norm_next = norm_now - 2.0 * alpha * crossed + alpha * alpha * squared
        direction = tuple((residual[k] + norm_next / norm_now * direction[k] for k in range(3)))
        norm_now = norm_next
    return (solution[0], solution[1], solution[2], direction[0], direction[1], direction[2])


def solution(mesh):
    in_specs = (
        P("dp", "mp"),
        P(None, None, "mp"),
        P(None, None, "mp"),
        P(None, "mp", None),
        P(None, "dp", "mp"),
        P(None, "dp", "mp"),
        P(None, "mp", "dp"),
        P(),
    )
    out_specs = (
        P(None, "dp", "mp"),
        P(None, "dp", "mp"),
        P(None, "mp", "dp"),
        P(None, "dp", "mp"),
        P(None, "dp", "mp"),
        P(None, "mp", "dp"),
    )
    return jax.shard_map(body, mesh=mesh, in_specs=in_specs, out_specs=out_specs, check_vma=False)
```

profile of v0, /device:TPU:0, one launch (start us, length us, event | category | flops | bytes accessed | tf_op | source)
XLA Modules:
  0.0 671.9 jit_solution(4627766731937684603)
XLA Ops:
  7.2 0.7 all-gather.6.cloned.1.call-update
  7.9 3.6 convert_element_type.67
  11.5 0.0 all-gather.8.cloned.1.call-start
  11.6 3.6 convert_element_type.66
  15.2 0.0 all-gather.12.cloned.1.call-start
  15.2 3.6 convert_element_type.70
  18.8 0.0 all-reduce.5.cloned.1.call-start
  18.8 46.0 %all-gather.6.cloned.1.call-done = bf16[256,2048]{1,0:T(8,128)(2,1)} async-done(((bf16[256,128]{1,0:T(8,128)(2,1)}), bf16[256,2048]{1,0:T(8,128)(2,1)}) %all-gather.6.cloned.1.call-update) | async-done | bytes 1048592 | tf_op jit(solution)/shard_map/all_gather | solution.py:49
  64.8 2.6 fusion.33
  67.4 2.4 multiply_convert_fusion.5
  69.8 0.4 copy-done.7
  70.2 2.1 fusion.27
  72.3 0.0 reduce-scatter.5.cloned.1.call-start
  72.3 6.6 all-gather.10.cloned.1.call-done
  78.9 2.2 fusion.65
  81.1 14.0 %all-gather.8.cloned.1.call-done = bf16[2,2048,448]{1,2,0:T(8,128)(2,1)} async-done(((bf16[2,1024,448]{1,2,0:T(8,128)(2,1)}), bf16[2,2048,448]{1,2,0:T(8,128)(2,1)}) %all-gather.8.cloned.1.call-update) | async-done | bytes 3670032 | tf_op jit(solution)/shard_map/all_gather | solution.py:62
  95.1 5.6 fusion.29
  100.8 10.4 %all-gather.12.cloned.1.call-done = bf16[2,448,2048]{2,1,0:T(8,128)(2,1)} async-done(((bf16[2,448,1024]{2,1,0:T(8,128)(2,1)}), bf16[2,448,2048]{2,1,0:T(8,128)(2,1)}) %all-gather.12.cloned.1.call-update) | async-done | bytes 3670032 | tf_op jit(solution)/shard_map/all_gather | solution.py:64
  111.2 2.9 convolution_add_fusion.2
  114.1 112.1 %all-reduce.8 = bf16[256,2048]{1,0:T(8,128)(2,1)} all-reduce(f32[256,2048]{1,0:T(8,128)S(1)} %convolution_add_fusion.2), channel_id=1, replica_groups=mesh['dp'=2,'mp'=16] {'mp'}, use_global_device_ids=true, to_apply=%region_4.0 | all-reduce | flops 524288 | bytes 3145728 | tf_op jit(solution)/shard_map/psum | solution.py:39
  226.1 37.1 %all-reduce.5.cloned.1.call-done = f32[256,2048]{1,0:T(8,128)} async-done(((f32[256,2048]{1,0:T(8,128)}), f32[256,2048]{1,0:T(8,128)}) %all-reduce.5.cloned.1.call-update) | async-done | bytes 2097168 | tf_op jit(solution)/shard_map/psum | solution.py:39
  263.2 2.0 add_convert_fusion.1
  265.2 0.6 copy-done.14
  265.8 0.7 fusion.23
  266.5 0.4 copy-done.16
  267.0 1.5 multiply_convert_fusion.4
  268.5 0.9 copy-done.20
  269.4 0.7 fusion.6
  270.1 1.5 fusion.60
  271.6 0.7 copy-done.21
  272.3 1.4 fusion.7
  273.8 6.2 fusion.12
  280.0 4.3 convolution_add_fusion.1
  284.3 0.0 all-gather.14.cloned.1.call-start
  284.3 80.9 %reduce-scatter.5.cloned.1.call-done = f32[256,128]{1,0:T(8,128)} async-done(((f32[256,2048]{1,0:T(8,128)}), f32[256,128]{1,0:T(8,128)}) %reduce-scatter.5.cloned.1.call-update) | async-done | bytes 131088 | tf_op jit(solution)/shard_map/reduce_scatter | solution.py:76
  365.2 1.6 add_convert_fusion.2
  366.8 49.5 %all-gather.14.cloned.1.call-done = bf16[256,2048]{1,0:T(8,128)(2,1)} async-done(((bf16[256,128]{1,0:T(8,128)(2,1)}), bf16[256,2048]{1,0:T(8,128)(2,1)}) %all-gather.14.cloned.1.call-update) | async-done | bytes 1048592 | tf_op jit(solution)/shard_map/all_gather | solution.py:79
  416.4 2.9 multiply_convert_fusion.2
  419.3 0.2 copy-done.15
  419.6 0.7 fusion.19
  420.3 1.3 copy-done.17
  421.6 2.1 convolution_add_fusion
  423.7 2.9 fusion.4
  426.6 122.9 %all-reduce.7.cloned.1.call-done = f32[256,2048]{1,0:T(8,128)} async-done(((f32[256,2048]{1,0:T(8,128)}), f32[256,2048]{1,0:T(8,128)}) %all-reduce.7.cloned.1.call-update) | async-done | bytes 2097168 | tf_op jit(solution)/shard_map/psum | solution.py:39
  549.5 3.0 fusion.25
  552.4 0.8 copy-done.6
  553.2 0.7 fusion
  554.0 2.2 pad_maximum_fusion
  556.1 0.3 reduce-scatter.9.cloned.1.call-start
  556.4 1.6 fusion.5
  558.0 1.8 fusion.1
  559.8 2.5 pad_maximum_fusion.1
  562.4 1.0 copy-done.11
  563.4 0.6 fusion.3
  564.0 2.4 fusion.2
  566.4 2.2 pad_maximum_fusion.2
  569.3 4.4 multiply_reduce_fusion.2
  573.7 9.0 %reduce-scatter.9.cloned.1.call-done = bf16[2,1024,448]{1,2,0:T(8,128)(2,1)} async-done(((bf16[2,2048,448]{1,2,0:T(8,128)(2,1)}), bf16[2,1024,448]{1,2,0:T(8,128)(2,1)}) %reduce-scatter.9.cloned.1.call-update) | async-done | bytes 1835024 | tf_op jit(solution)/shard_map/reduce_scatter | solution.py:101
  582.7 4.4 multiply_reduce_fusion.1
  588.6 10.0 %reduce-scatter.11.cloned.1.call-done = bf16[2,448,1024]{2,1,0:T(8,128)(2,1)} async-done(((bf16[2,448,2048]{2,1,0:T(8,128)(2,1)}), bf16[2,448,1024]{2,1,0:T(8,128)(2,1)}) %reduce-scatter.11.cloned.1.call-update) | async-done | bytes 1835024 | tf_op jit(solution)/shard_map/reduce_scatter | solution.py:107
  598.5 4.4 multiply_reduce_fusion
  607.4 40.6 %all-reduce = (f32[]{:T(128)}, f32[]{:T(128)}, f32[]{:T(128)}) all-reduce(f32[]{:T(128)S(6)} %add.108, f32[]{:T(128)S(6)} %add.128, f32[]{:T(128)S(6)} %add.130), channel_id=1, replica_groups=mesh['dp'=2,'mp'=16] {'dp','mp'}, use_global_device_ids=true, to_apply=%region_3.0 | all-reduce | flops 3 | bytes 24 | tf_op jit(solution)/shard_map/psum | solution.py:124
  652.0 9.2 %multiply_add_fusion.1 = (f32[2,1024,448]{1,2,0:T(8,128)}, f32[2,1024,448]{1,2,0:T(8,128)}, f32[2,1024,448]{1,2,0:T(8,128)}, f32[2,1024,448]{1,2,0:T(8,128)}) fusion(f32[2,1024,448]{1,2,0:T(8,128)} %param.13, bf16[2,1024,448]{1,2,0:T(8,128)(2,1)} %reduce-scatter.9.cloned.1.call-done, f32[]{:T(128)S(6)} %div.17, f32[]{:T(128)S(6)} %div.16, f32[]{:T(128)} %bitcast.123, ...), kind=kLoop, calls=%fused_computation.4 | loop fusion | flops 16515072 | bytes 25690124 | tf_op jit(solution)/shard_map/add | solution.py:139
  661.2 4.1 multiply_add_fusion
  (53 shorter events, 0.5 us)
Async XLA Ops:
  7.2 57.6 %all-gather.6.cloned.1.call-start = ((), (), s32[]{:S(2)}) async-start(), calls=%async_computation.4 | async-start | bytes 1114112 | tf_op jit(solution)/shard_map/all_gather | solution.py:49
  7.9 71.0 %all-gather.10.cloned.1.call-start = ((), (), s32[]{:S(2)}) async-start(), calls=%async_computation.6 | async-start | bytes 5505024 | tf_op jit(solution)/shard_map/all_gather | solution.py:63
  11.5 83.6 %all-gather.8.cloned.1.call-start = ((), (), s32[]{:S(2)}) async-start(), calls=%async_computation.5 | async-start | bytes 5505024 | tf_op jit(solution)/shard_map/all_gather | solution.py:62
  15.2 96.0 %all-gather.12.cloned.1.call-start = ((), (), s32[]{:S(2)}) async-start(), calls=%async_computation.7 | async-start | bytes 5505024 | tf_op jit(solution)/shard_map/all_gather | solution.py:64
  18.8 244.4 %all-reduce.5.cloned.1.call-start = ((), (), s32[]{:S(2)}) async-start(), calls=%async_computation.8 | async-start | bytes 4194304 | tf_op jit(solution)/shard_map/psum | solution.py:39
  64.8 2.6 copy-start.2
  67.4 27.7 %copy-start.8 = (f32[256,448]{0,1:T(8,128)}, f32[256,448]{0,1:T(8,128)S(1)}, u32[]{:S(2)}) copy-start(f32[256,448]{0,1:T(8,128)S(1)} %fusion.33) | copy-start | bytes 1376260
  67.4 2.8 copy-start.7
  69.8 25.3 %copy-start.18 = (f32[256,448]{0,1:T(8,128)}, f32[256,448]{0,1:T(8,128)S(1)}, u32[]{:S(2)}) copy-start(f32[256,448]{0,1:T(8,128)S(1)} %get-tuple-element.27) | copy-start | bytes 1376260
  72.3 293.0 %reduce-scatter.5.cloned.1.call-start = ((), (), s32[]{:S(2)}) async-start(), calls=%async_computation.9 | async-start | bytes 2228224 | tf_op jit(solution)/shard_map/reduce_scatter | solution.py:76
  263.2 2.7 copy-start.14
  263.2 3.8 copy-start.16
  267.0 3.1 copy-start.22
  267.0 2.5 copy-start.20
  267.0 3.1 copy-start.10
  270.1 2.2 copy-start.21
  284.3 132.1 %all-gather.14.cloned.1.call-start = ((), (), s32[]{:S(2)}) async-start(), calls=%async_computation.10 | async-start | bytes 1114112 | tf_op jit(solution)/shard_map/all_gather | solution.py:79
  366.8 182.6 %all-reduce.7.cloned.1.call-start = ((), (), s32[]{:S(2)}) async-start(), calls=%async_computation.11 | async-start | bytes 4194304 | tf_op jit(solution)/shard_map/psum | solution.py:39
  416.4 3.2 copy-start.15
  419.3 1.0 copy-start.12
  419.3 1.0 copy-start.13
  419.3 2.3 copy-start.17
  423.6 125.8 %copy-start.1 = (bf16[256,2048]{1,0:T(8,128)(2,1)S(1)}, bf16[256,2048]{1,0:T(8,128)(2,1)}, u32[]{:S(2)}) copy-start(bf16[256,2048]{1,0:T(8,128)(2,1)} %all-gather.14.cloned.1.call-done) | copy-start | bytes 3145732
  423.6 145.7 %reduce-scatter.7.cloned.1.call-start = ((), (), s32[]{:S(2)}) async-start(), calls=%async_computation.12 | async-start | bytes 5505024 | tf_op jit(solution)/shard_map/reduce_scatter | solution.py:95
  549.4 3.8 copy-start.9
  549.4 3.8 copy-start.19
  549.5 4.5 copy-start.4
  552.4 0.8 copy-start.6
  556.1 26.6 %reduce-scatter.9.cloned.1.call-start = ((), (), s32[]{:S(2)}) async-start(), calls=%async_computation.13 | async-start | bytes 5505024 | tf_op jit(solution)/shard_map/reduce_scatter | solution.py:101
  562.3 1.0 copy-start.11
  562.4 36.2 %reduce-scatter.11.cloned.1.call-start = ((), (), s32[]{:S(2)}) async-start(), calls=%async_computation.14 | async-start | bytes 5505024 | tf_op jit(solution)/shard_map/reduce_scatter | solution.py:107
  587.2 64.8 %copy-start.3 = (bf16[2,1024,448]{1,2,0:T(8,128)(2,1)S(1)}, bf16[2,1024,448]{1,2,0:T(8,128)(2,1)}, u32[]{:S(2)}) copy-start(bf16[2,1024,448]{1,2,0:T(8,128)(2,1)} %reduce-scatter.7.cloned.1.call-done) | copy-start | bytes 5505028
  652.0 9.2 %copy-start = (f32[2,448,1024]{2,1,0:T(8,128)S(1)}, f32[2,448,1024]{2,1,0:T(8,128)}, u32[]{:S(2)}) copy-start(f32[2,448,1024]{2,1,0:T(8,128)} %param.14) | copy-start | bytes 11010052
  652.0 9.2 %copy-start.5 = (bf16[2,448,1024]{2,1,0:T(8,128)(2,1)S(1)}, bf16[2,448,1024]{2,1,0:T(8,128)(2,1)}, u32[]{:S(2)}) copy-start(bf16[2,448,1024]{2,1,0:T(8,128)(2,1)} %reduce-scatter.11.cloned.1.call-done) | copy-start | bytes 5505028
Sparse Core Ops, SparseCore 0:
  10.7 54.0 all-gather.5
  66.9 11.8 all-gather.9
  81.0 14.0 all-gather.7
  97.1 14.0 all-gather.11
  117.1 146.0 all-reduce.4
  284.4 80.7 reduce-scatter.4
  368.5 47.8 all-gather.13
  423.8 125.6 all-reduce.6
  556.3 10.8 reduce-scatter.6
  569.8 12.9 reduce-scatter.8
  585.6 12.8 reduce-scatter.10
where the time goes:
time: 673 us; the launch traced here: 672 us
  waiting for transfers between devices  387 us (58%)
  blocking collectives  153 us (23%)
  matrix products  52.7 us (8%)
  other arithmetic  47.6 us (7%)
  between operations  24.7 us (4%)
    psum x2, waiting for transfers between devices, finish_first(): summed = lax.psum(partial_value, 'mp')  160 us
    psum x1, blocking collectives, finish_first(): summed = lax.psum(partial_value, 'mp')  112 us
    reduce_scatter x1, waiting for transfers between devices, curvature(): lax.psum_scatter(second_partial, 'mp', scatter_dimension=1, tiled=True)  80.9 us
    all_gather x1, waiting for transfers between devices, curvature(): cotan = lax.all_gather(cotan_share, 'mp', axis=1, tiled=True)  49.5 us
    all_gather x1, waiting for transfers between devices, body(): tokens_whole = lax.all_gather(tokens, 'mp', axis=1, tiled=True)  46 us
    psum x1, blocking collectives, body(): norm_now = lax.psum(local_inner(residual, residual), ('dp', 'mp'))  40.6 us
    dot_general x13, matrix products, matmul(): return jnp.dot(left, right, preferred_element_type=jnp.float32)  34 us
    all_gather x1, waiting for transfers between devices, curvature(): lax.all_gather(vectors[0].astype(jnp.bfloat16), 'dp', axis=1, tiled=True)  14 us
  transfers between devices with their start and end apart: 11, of which 10 were waited for; matrix products, arithmetic and copies ran while one was open for 8% of the time, Pallas kernels for 0%

commit v1 on v0

--- a/solution.py
+++ b/solution.py
@@ -36,7 +36,9 @@
 
 
 def finish_first(partial_value, whole_add):
-    summed = lax.psum(partial_value, "mp")
+    summed = partial_value
+    for hop in (1, 2, 4, 8):
+        summed = summed + lax.ppermute(summed, "mp", [(dev, dev ^ hop) for dev in range(16)])
     if whole_add is not None:
         summed = summed + whole_add.astype(jnp.float32)
     return summed.astype(jnp.bfloat16)

time: 673 us -> 898 us (1.33)
  waiting for transfers between devices: 387 us -> 715 us
  blocking collectives: 153 us -> 40.6 us
  starting transfers between devices: 0.67 us -> 14.4 us
    ppermute x0 -> x12, waiting for transfers between devices: none -> 486 us  [finish_first(): lax.ppermute(summed, 'mp', [(dev, dev ^ hop) for dev in range(16)])]
    psum x2 -> x0, waiting for transfers between devices: 160 us -> none  [finish_first(): summed = lax.psum(partial_value, 'mp')]
    psum x1 -> x0, blocking collectives: 112 us -> none  [finish_first(): summed = lax.psum(partial_value, 'mp')]
    ppermute x0 -> x12, starting transfers between devices: none -> 13.9 us  [finish_first(): lax.ppermute(summed, 'mp', [(dev, dev ^ hop) for dev in range(16)])]
  transfers between devices with their start and end apart: 11 -> 21, of which waited for: 10 -> 20; matrix products, arithmetic and copies ran while one was open for 8% -> 6% of each run, Pallas kernels for 0% -> 0%
where the time goes in v1:
time: 898 us
  waiting for transfers between devices  715 us (80%)
  other arithmetic  51.8 us (6%)
  matrix products  45.4 us (5%)
  blocking collectives  40.6 us (5%)
  between operations  24.8 us (3%)
  starting transfers between devices  14.4 us (2%)
    ppermute x12, waiting for transfers between devices, finish_first(): lax.ppermute(summed, 'mp', [(dev, dev ^ hop) for dev in range(16)])  486 us
    reduce_scatter x1, waiting for transfers between devices, curvature(): lax.psum_scatter(second_partial, 'mp', scatter_dimension=1, tiled=True)  81 us
    all_gather x1, waiting for transfers between devices, curvature(): cotan = lax.all_gather(cotan_share, 'mp', axis=1, tiled=True)  49.4 us
    all_gather x1, waiting for transfers between devices, body(): tokens_whole = lax.all_gather(tokens, 'mp', axis=1, tiled=True)  46 us
    psum x1, blocking collectives, body(): norm_now = lax.psum(local_inner(residual, residual), ('dp', 'mp'))  40.6 us
    dot_general x13, matrix products, matmul(): return jnp.dot(left, right, preferred_element_type=jnp.float32)  34.3 us
  transfers between devices with their start and end apart: 21, of which 20 were waited for; matrix products, arithmetic and copies ran while one was open for 6% of the time, Pallas kernels for 0%

profile of v1, /device:TPU:0, one launch (start us, length us, event | category | flops | bytes accessed | tf_op | source)
XLA Modules:
  0.0 897.7 jit_solution(188079672889287025)
XLA Ops:
  7.9 3.6 convert_element_type.67
  11.6 3.6 convert_element_type.66
  15.2 3.6 convert_element_type.70
  18.8 46.0 %all-gather.6.cloned.1.call-done = bf16[256,2048]{1,0:T(8,128)(2,1)} async-done(((bf16[256,128]{1,0:T(8,128)(2,1)}), bf16[256,2048]{1,0:T(8,128)(2,1)}) %all-gather.6.cloned.1.call-update) | async-done | bytes 1048592 | tf_op jit(solution)/shard_map/all_gather | solution.py:51
  64.8 2.6 fusion.33
  67.4 2.4 multiply_convert_fusion.5
  70.2 2.1 fusion.27
  72.2 1.1 collective-permute-start.4
  73.3 5.5 all-gather.10.cloned.1.call-done
  78.9 2.2 fusion.59
  81.1 14.0 %all-gather.8.cloned.1.call-done = bf16[2,2048,448]{1,2,0:T(8,128)(2,1)} async-done(((bf16[2,1024,448]{1,2,0:T(8,128)(2,1)}), bf16[2,2048,448]{1,2,0:T(8,128)(2,1)}) %all-gather.8.cloned.1.call-update) | async-done | bytes 3670032 | tf_op jit(solution)/shard_map/all_gather | solution.py:64
  95.1 5.6 fusion.29
  100.8 10.4 %all-gather.12.cloned.1.call-done = bf16[2,448,2048]{2,1,0:T(8,128)(2,1)} async-done(((bf16[2,448,1024]{2,1,0:T(8,128)(2,1)}), bf16[2,448,2048]{2,1,0:T(8,128)(2,1)}) %all-gather.12.cloned.1.call-update) | async-done | bytes 3670032 | tf_op jit(solution)/shard_map/all_gather | solution.py:66
  111.2 2.9 convolution_add_fusion.2
  114.1 1.8 collective-permute-start
  115.9 5.2 collective-permute-done.4
  121.0 2.5 add.148
  123.5 1.7 collective-permute-start.5
  125.2 38.9 %collective-permute-done = f32[256,2048]{1,0:T(8,128)S(1)} collective-permute-done((f32[256,2048]{1,0:T(8,128)S(1)}, f32[256,2048]{1,0:T(8,128)S(1)}, u32[]{:S(2)}, u32[]{:S(2)}) %collective-permute-start) | collective-permute-done | bytes 2097184 | tf_op jit(solution)/shard_map/ppermute | solution.py:41
  164.4 1.6 collective-permute-start.1
  166.0 3.9 collective-permute-done.5
  170.3 42.3 %collective-permute-done.1 = f32[256,2048]{1,0:T(8,128)S(1)} collective-permute-done((f32[256,2048]{1,0:T(8,128)S(1)}, f32[256,2048]{1,0:T(8,128)S(1)}, u32[]{:S(2)}, u32[]{:S(2)}) %collective-permute-start.1) | collective-permute-done | bytes 2097184 | tf_op jit(solution)/shard_map/ppermute | solution.py:41
  213.4 2.2 collective-permute-start.7
  215.6 87.4 %collective-permute-done.2 = f32[256,2048]{1,0:T(8,128)S(1)} collective-permute-done((f32[256,2048]{1,0:T(8,128)S(1)}, f32[256,2048]{1,0:T(8,128)S(1)}, u32[]{:S(2)}, u32[]{:S(2)}) %collective-permute-start.2) | collective-permute-done | bytes 2097184 | tf_op jit(solution)/shard_map/ppermute | solution.py:41
  303.4 47.4 %collective-permute-done.7 = f32[256,2048]{1,0:T(8,128)S(1)} collective-permute-done((f32[256,2048]{1,0:T(8,128)S(1)}, f32[256,2048]{1,0:T(8,128)S(1)}, u32[]{:S(2)}, u32[]{:S(2)}) %collective-permute-start.7) | collective-permute-done | bytes 2097184 | tf_op jit(solution)/shard_map/ppermute | solution.py:41
  352.8 0.8 copy-done.21
  353.6 1.4 fusion.7
  355.1 1.6 multiply_convert_fusion.4
  356.6 38.8 %collective-permute-done.3 = f32[256,2048]{1,0:T(8,128)S(1)} collective-permute-done((f32[256,2048]{1,0:T(8,128)S(1)}, f32[256,2048]{1,0:T(8,128)S(1)}, u32[]{:S(2)}, u32[]{:S(2)}) %collective-permute-start.3) | collective-permute-done | bytes 2097184 | tf_op jit(solution)/shard_map/ppermute | solution.py:41
  395.8 1.5 fusion.54
  397.3 6.4 fusion.12
  403.7 4.3 convolution_add_fusion.1
  408.1 81.0 %reduce-scatter.5.cloned.1.call-done = f32[256,128]{1,0:T(8,128)} async-done(((f32[256,2048]{1,0:T(8,128)}), f32[256,128]{1,0:T(8,128)}) %reduce-scatter.5.cloned.1.call-update) | async-done | bytes 131088 | tf_op jit(solution)/shard_map/reduce_scatter | solution.py:78
  489.1 1.6 add_convert_fusion.5
  490.7 49.4 %all-gather.14.cloned.1.call-done = bf16[256,2048]{1,0:T(8,128)(2,1)} async-done(((bf16[256,128]{1,0:T(8,128)(2,1)}), bf16[256,2048]{1,0:T(8,128)(2,1)}) %all-gather.14.cloned.1.call-update) | async-done | bytes 1048592 | tf_op jit(solution)/shard_map/all_gather | solution.py:81
  540.1 2.9 multiply_convert_fusion.2
  543.2 0.7 fusion.19
  544.0 1.2 copy-done.15
  545.2 0.7 convolution_add_fusion
  545.9 1.2 collective-permute-start.8
  547.1 45.6 %collective-permute-done.8 = f32[256,2048]{1,0:T(8,128)S(1)} collective-permute-done((f32[256,2048]{1,0:T(8,128)S(1)}, f32[256,2048]{1,0:T(8,128)S(1)}, u32[]{:S(2)}, u32[]{:S(2)}) %collective-permute-start.8) | collective-permute-done | bytes 2097184 | tf_op jit(solution)/shard_map/ppermute | solution.py:41
  593.0 1.6 collective-permute-start.9
  594.6 44.3 %collective-permute-done.9 = f32[256,2048]{1,0:T(8,128)S(1)} collective-permute-done((f32[256,2048]{1,0:T(8,128)S(1)}, f32[256,2048]{1,0:T(8,128)S(1)}, u32[]{:S(2)}, u32[]{:S(2)}) %collective-permute-start.9) | collective-permute-done | bytes 2097184 | tf_op jit(solution)/shard_map/ppermute | solution.py:41
  639.3 45.0 %collective-permute-done.10 = f32[256,2048]{1,0:T(8,128)S(1)} collective-permute-done((f32[256,2048]{1,0:T(8,128)S(1)}, f32[256,2048]{1,0:T(8,128)S(1)}, u32[]{:S(2)}, u32[]{:S(2)}) %collective-permute-start.10) | collective-permute-done | bytes 2097184 | tf_op jit(solution)/shard_map/ppermute | solution.py:41
  684.7 2.4 collective-permute-start.11
  687.7 87.0 %collective-permute-done.11 = f32[256,2048]{1,0:T(8,128)S(1)} collective-permute-done((f32[256,2048]{1,0:T(8,128)S(1)}, f32[256,2048]{1,0:T(8,128)S(1)}, u32[]{:S(2)}, u32[]{:S(2)}) %collective-permute-start.11) | collective-permute-done | bytes 2097184 | tf_op jit(solution)/shard_map/ppermute | solution.py:41
  775.3 1.0 copy-done.5
  776.9 0.8 copy-done.9
  777.7 0.7 fusion
  778.4 2.2 pad_maximum_fusion
  780.7 1.6 fusion.5
  782.3 1.8 fusion.1
  784.1 2.2 pad_maximum_fusion.1
  786.6 0.7 copy-done.10
  788.7 2.2 pad_maximum_fusion.2
  791.5 1.2 reduce-scatter.7.cloned.1.call-done
  792.7 4.4 multiply_reduce_fusion.2
  797.1 11.4 %reduce-scatter.9.cloned.1.call-done = bf16[2,1024,448]{1,2,0:T(8,128)(2,1)} async-done(((bf16[2,2048,448]{1,2,0:T(8,128)(2,1)}), bf16[2,1024,448]{1,2,0:T(8,128)(2,1)}) %reduce-scatter.9.cloned.1.call-update) | async-done | bytes 1835024 | tf_op jit(solution)/shard_map/reduce_scatter | solution.py:103
  808.5 4.4 multiply_reduce_fusion.1
  814.3 9.9 %reduce-scatter.11.cloned.1.call-done = bf16[2,448,1024]{2,1,0:T(8,128)(2,1)} async-done(((bf16[2,448,2048]{2,1,0:T(8,128)(2,1)}), bf16[2,448,1024]{2,1,0:T(8,128)(2,1)}) %reduce-scatter.11.cloned.1.call-update) | async-done | bytes 1835024 | tf_op jit(solution)/shard_map/reduce_scatter | solution.py:109
  824.3 4.4 multiply_reduce_fusion
  833.2 40.6 %all-reduce = (f32[]{:T(128)}, f32[]{:T(128)}, f32[]{:T(128)}) all-reduce(f32[]{:T(128)S(6)} %add.138, f32[]{:T(128)S(6)} %add.170, f32[]{:T(128)S(6)} %add.172), channel_id=1, replica_groups=mesh['dp'=2,'mp'=16] {'dp','mp'}, use_global_device_ids=true, to_apply=%region_3.0 | all-reduce | flops 3 | bytes 24 | tf_op jit(solution)/shard_map/psum | solution.py:126
  877.8 9.2 %multiply_add_fusion.1 = (f32[2,1024,448]{1,2,0:T(8,128)}, f32[2,1024,448]{1,2,0:T(8,128)}, f32[2,1024,448]{1,2,0:T(8,128)}, f32[2,1024,448]{1,2,0:T(8,128)}) fusion(f32[2,1024,448]{1,2,0:T(8,128)} %param.13, bf16[2,1024,448]{1,2,0:T(8,128)(2,1)} %reduce-scatter.9.cloned.1.call-done, f32[]{:T(128)S(6)} %div.17, f32[]{:T(128)S(6)} %div.16, f32[]{:T(128)} %bitcast.121, ...), kind=kLoop, calls=%fused_computation.4 | loop fusion | flops 16515072 | bytes 25690124 | tf_op jit(solution)/shard_map/add | solution.py:141
  887.0 4.1 multiply_add_fusion
  (81 shorter events, 10.5 us)
Async XLA Ops:
  7.2 57.6 %all-gather.6.cloned.1.call-start = ((), (), s32[]{:S(2)}) async-start(), calls=%async_computation.4 | async-start | bytes 1114112 | tf_op jit(solution)/shard_map/all_gather | solution.py:51
  7.9 71.0 %all-gather.10.cloned.1.call-start = ((), (), s32[]{:S(2)}) async-start(), calls=%async_computation.6 | async-start | bytes 5505024 | tf_op jit(solution)/shard_map/all_gather | solution.py:65
  11.5 83.6 %all-gather.8.cloned.1.call-start = ((), (), s32[]{:S(2)}) async-start(), calls=%async_computation.5 | async-start | bytes 5505024 | tf_op jit(solution)/shard_map/all_gather | solution.py:64
  15.2 96.0 %all-gather.12.cloned.1.call-start = ((), (), s32[]{:S(2)}) async-start(), calls=%async_computation.7 | async-start | bytes 5505024 | tf_op jit(solution)/shard_map/all_gather | solution.py:66
  18.8 470.3 %reduce-scatter.5.cloned.1.call-start = ((), (), s32[]{:S(2)}) async-start(), calls=%async_computation.8 | async-start | bytes 2228224 | tf_op jit(solution)/shard_map/reduce_scatter | solution.py:78
  64.8 2.6 copy-start.1
  67.4 27.7 %copy-start.7 = (f32[256,448]{0,1:T(8,128)}, f32[256,448]{0,1:T(8,128)S(1)}, u32[]{:S(2)}) copy-start(f32[256,448]{0,1:T(8,128)S(1)} %fusion.33) | copy-start | bytes 1376260
  67.4 2.8 copy-start.16
  69.8 25.3 %copy-start.18 = (f32[256,448]{0,1:T(8,128)}, f32[256,448]{0,1:T(8,128)S(1)}, u32[]{:S(2)}) copy-start(f32[256,448]{0,1:T(8,128)S(1)} %get-tuple-element.27) | copy-start | bytes 1376260
  72.2 48.8 %collective-permute-start.4 = (f32[256,2048]{1,0:T(8,128)}, f32[256,2048]{1,0:T(8,128)}, u32[]{:S(2)}, u32[]{:S(2)}) collective-permute-start(f32[256,2048]{1,0:T(8,128)} %fusion.27), channel_id=1, source_target_pairs={{0,1},{1,0},{2,3},{3,2},{4,5},{5,4},{6,7},{7,6},{8,9},{9,8},{10,11... | collective-permute-start | bytes 6291464 | tf_op jit(solution)/shard_map/ppermute | solution.py:41
  114.1 50.0 %collective-permute-start = (f32[256,2048]{1,0:T(8,128)S(1)}, f32[256,2048]{1,0:T(8,128)S(1)}, u32[]{:S(2)}, u32[]{:S(2)}) collective-permute-start(f32[256,2048]{1,0:T(8,128)S(1)} %convolution_add_fusion.2), channel_id=1, source_target_pairs={{0,1},{1,0},{2,3},{3,2},{4,5},{5,4},{6,7},{7,6},{8,9},{9,8},{10,11... | collective-permute-start | bytes 6291464 | tf_op jit(solution)/shard_map/ppermute | solution.py:41
  123.5 46.4 %collective-permute-start.5 = (f32[256,2048]{1,0:T(8,128)S(1)}, f32[256,2048]{1,0:T(8,128)S(1)}, u32[]{:S(2)}, u32[]{:S(2)}) collective-permute-start(f32[256,2048]{1,0:T(8,128)S(1)} %add.148), channel_id=1, source_target_pairs={{0,2},{1,3},{2,0},{3,1},{4,6},{5,7},{6,4},{7,5},{8,10},{9,11},{10,... | collective-permute-start | bytes 6291464 | tf_op jit(solution)/shard_map/ppermute | solution.py:41
  164.4 48.2 %collective-permute-start.1 = (f32[256,2048]{1,0:T(8,128)S(1)}, f32[256,2048]{1,0:T(8,128)S(1)}, u32[]{:S(2)}, u32[]{:S(2)}) collective-permute-start(f32[256,2048]{1,0:T(8,128)S(1)} %add.143), channel_id=1, source_target_pairs={{0,2},{1,3},{2,0},{3,1},{4,6},{5,7},{6,4},{7,5},{8,10},{9,11},{10,... | collective-permute-start | bytes 6291464 | tf_op jit(solution)/shard_map/ppermute | solution.py:41
  170.2 42.8 %collective-permute-start.6 = (f32[256,2048]{1,0:T(8,128)S(1)}, f32[256,2048]{1,0:T(8,128)S(1)}, u32[]{:S(2)}, u32[]{:S(2)}) collective-permute-start(f32[256,2048]{1,0:T(8,128)S(1)} %add.149), channel_id=1, source_target_pairs={{0,4},{1,5},{2,6},{3,7},{4,0},{5,1},{6,2},{7,3},{8,12},{9,13},{10,... | collective-permute-start | bytes 6291464 | tf_op jit(solution)/shard_map/ppermute | solution.py:41
  212.9 90.1 %collective-permute-start.2 = (f32[256,2048]{1,0:T(8,128)S(1)}, f32[256,2048]{1,0:T(8,128)S(1)}, u32[]{:S(2)}, u32[]{:S(2)}) collective-permute-start(f32[256,2048]{1,0:T(8,128)S(1)} %add.144), channel_id=1, source_target_pairs={{0,4},{1,5},{2,6},{3,7},{4,0},{5,1},{6,2},{7,3},{8,12},{9,13},{10,... | collective-permute-start | bytes 6291464 | tf_op jit(solution)/shard_map/ppermute | solution.py:41
  213.4 137.5 %collective-permute-start.7 = (f32[256,2048]{1,0:T(8,128)S(1)}, f32[256,2048]{1,0:T(8,128)S(1)}, u32[]{:S(2)}, u32[]{:S(2)}) collective-permute-start(f32[256,2048]{1,0:T(8,128)S(1)} %add.150), channel_id=1, source_target_pairs={{0,8},{1,9},{2,10},{3,11},{4,12},{5,13},{6,14},{7,15},{8,0},{9,1},... | collective-permute-start | bytes 6291464 | tf_op jit(solution)/shard_map/ppermute | solution.py:41
  303.3 48.1 %copy-start.12 = (bf16[2,2048,448]{1,2,0:T(8,128)(2,1)S(1)}, bf16[2,2048,448]{1,2,0:T(8,128)(2,1)}, u32[]{:S(2)}) copy-start(bf16[2,2048,448]{1,2,0:T(8,128)(2,1)} %param.9) | copy-start | bytes 11010052
  303.3 48.8 %copy-start.20 = (bf16[2,2048,448]{1,2,0:T(8,128)(2,1)S(1)}, bf16[2,2048,448]{1,2,0:T(8,128)(2,1)}, u32[]{:S(2)}) copy-start(bf16[2,2048,448]{1,2,0:T(8,128)(2,1)} %all-gather.10.cloned.1.call-done) | copy-start | bytes 11010052
  303.3 92.1 %collective-permute-start.3 = (f32[256,2048]{1,0:T(8,128)S(1)}, f32[256,2048]{1,0:T(8,128)S(1)}, u32[]{:S(2)}, u32[]{:S(2)}) collective-permute-start(f32[256,2048]{1,0:T(8,128)S(1)} %add.145), channel_id=1, source_target_pairs={{0,8},{1,9},{2,10},{3,11},{4,12},{5,13},{6,14},{7,15},{8,0},{9,1},... | collective-permute-start | bytes 6291464 | tf_op jit(solution)/shard_map/ppermute | solution.py:41
  351.4 2.2 copy-start.21
  352.1 43.7 %copy-start.22 = (f32[256,448]{0,1:T(8,128)}, f32[256,448]{0,1:T(8,128)S(1)}, u32[]{:S(2)}) copy-start(f32[256,448]{0,1:T(8,128)S(1)} %fusion.23) | copy-start | bytes 1376260
  352.1 2.9 copy-start.14
  408.0 132.0 %all-gather.14.cloned.1.call-start = ((), (), s32[]{:S(2)}) async-start(), calls=%async_computation.9 | async-start | bytes 1114112 | tf_op jit(solution)/shard_map/all_gather | solution.py:81
  490.7 302.1 %reduce-scatter.7.cloned.1.call-start = ((), (), s32[]{:S(2)}) async-start(), calls=%async_computation.10 | async-start | bytes 5505024 | tf_op jit(solution)/shard_map/reduce_scatter | solution.py:97
  540.1 3.2 copy-start.13
  543.0 3.0 copy-start.11
  543.0 2.2 copy-start.15
  545.9 46.8 %collective-permute-start.8 = (f32[256,2048]{1,0:T(8,128)S(1)}, f32[256,2048]{1,0:T(8,128)S(1)}, u32[]{:S(2)}, u32[]{:S(2)}) collective-permute-start(f32[256,2048]{1,0:T(8,128)S(1)} %convolution_add_fusion), channel_id=1, source_target_pairs={{0,1},{1,0},{2,3},{3,2},{4,5},{5,4},{6,7},{7,6},{8,9},{9,8},{10,11... | collective-permute-start | bytes 6291464 | tf_op jit(solution)/shard_map/ppermute | solution.py:41
  593.0 45.9 %collective-permute-start.9 = (f32[256,2048]{1,0:T(8,128)S(1)}, f32[256,2048]{1,0:T(8,128)S(1)}, u32[]{:S(2)}, u32[]{:S(2)}) collective-permute-start(f32[256,2048]{1,0:T(8,128)S(1)} %add.161), channel_id=1, source_target_pairs={{0,2},{1,3},{2,0},{3,1},{4,6},{5,7},{6,4},{7,5},{8,10},{9,11},{10,... | collective-permute-start | bytes 6291464 | tf_op jit(solution)/shard_map/ppermute | solution.py:41
  639.3 135.5 %copy-start.4 = (bf16[256,2048]{1,0:T(8,128)(2,1)S(1)}, bf16[256,2048]{1,0:T(8,128)(2,1)}, u32[]{:S(2)}) copy-start(bf16[256,2048]{1,0:T(8,128)(2,1)} %all-gather.14.cloned.1.call-done) | copy-start | bytes 3145732
  639.3 45.1 %collective-permute-start.10 = (f32[256,2048]{1,0:T(8,128)S(1)}, f32[256,2048]{1,0:T(8,128)S(1)}, u32[]{:S(2)}, u32[]{:S(2)}) collective-permute-start(f32[256,2048]{1,0:T(8,128)S(1)} %add.162), channel_id=1, source_target_pairs={{0,4},{1,5},{2,6},{3,7},{4,0},{5,1},{6,2},{7,3},{8,12},{9,13},{10,... | collective-permute-start | bytes 6291464 | tf_op jit(solution)/shard_map/ppermute | solution.py:41
  684.7 90.0 %collective-permute-start.11 = (f32[256,2048]{1,0:T(8,128)S(1)}, f32[256,2048]{1,0:T(8,128)S(1)}, u32[]{:S(2)}, u32[]{:S(2)}) collective-permute-start(f32[256,2048]{1,0:T(8,128)S(1)} %add.163), channel_id=1, source_target_pairs={{0,8},{1,9},{2,10},{3,11},{4,12},{5,13},{6,14},{7,15},{8,0},{9,1},... | collective-permute-start | bytes 6291464 | tf_op jit(solution)/shard_map/ppermute | solution.py:41
  687.7 88.5 %copy-start.17 = (bf16[2,448,2048]{2,1,0:T(8,128)(2,1)S(1)}, bf16[2,448,2048]{2,1,0:T(8,128)(2,1)}, u32[]{:S(2)}) copy-start(bf16[2,448,2048]{2,1,0:T(8,128)(2,1)} %param.11) | copy-start | bytes 11010052
  687.7 90.0 %copy-start.8 = (f32[256,448]{0,1:T(8,128)S(1)}, f32[256,448]{0,1:T(8,128)}, u32[]{:S(2)}) copy-start(f32[256,448]{0,1:T(8,128)} %copy-done.7) | copy-start | bytes 1376260
  687.7 90.0 %copy-start.19 = (f32[256,448]{0,1:T(8,128)S(1)}, f32[256,448]{0,1:T(8,128)}, u32[]{:S(2)}) copy-start(f32[256,448]{0,1:T(8,128)} %copy-done.18) | copy-start | bytes 1376260
  775.3 1.0 copy-start.5
  776.9 0.8 copy-start.9
  780.6 27.9 %reduce-scatter.9.cloned.1.call-start = ((), (), s32[]{:S(2)}) async-start(), calls=%async_computation.11 | async-start | bytes 5505024 | tf_op jit(solution)/shard_map/reduce_scatter | solution.py:103
  786.3 1.0 copy-start.10
  786.3 1.8 copy-start.6
  786.3 38.0 %reduce-scatter.11.cloned.1.call-start = ((), (), s32[]{:S(2)}) async-start(), calls=%async_computation.12 | async-start | bytes 5505024 | tf_op jit(solution)/shard_map/reduce_scatter | solution.py:109
  812.9 64.8 %copy-start.2 = (bf16[2,1024,448]{1,2,0:T(8,128)(2,1)S(1)}, bf16[2,1024,448]{1,2,0:T(8,128)(2,1)}, u32[]{:S(2)}) copy-start(bf16[2,1024,448]{1,2,0:T(8,128)(2,1)} %reduce-scatter.7.cloned.1.call-done) | copy-start | bytes 5505028
  877.8 9.2 %copy-start = (f32[2,448,1024]{2,1,0:T(8,128)S(1)}, f32[2,448,1024]{2,1,0:T(8,128)}, u32[]{:S(2)}) copy-start(f32[2,448,1024]{2,1,0:T(8,128)} %param.14) | copy-start | bytes 11010052
  877.8 9.2 %copy-start.3 = (bf16[2,448,1024]{2,1,0:T(8,128)(2,1)S(1)}, bf16[2,448,1024]{2,1,0:T(8,128)(2,1)}, u32[]{:S(2)}) copy-start(bf16[2,448,1024]{2,1,0:T(8,128)(2,1)} %reduce-scatter.11.cloned.1.call-done) | copy-start | bytes 5505028
Sparse Core Ops, SparseCore 0:
  10.7 54.0 all-gather.5
  66.9 11.8 all-gather.9
  81.0 14.0 all-gather.7
  97.1 14.0 all-gather.11
  408.1 80.8 reduce-scatter.4
  492.2 47.8 all-gather.13
  780.7 11.9 reduce-scatter.6
  795.6 12.8 reduce-scatter.8
  811.3 12.8 reduce-scatter.10
